TPU v7x, 32 devices: a whole 2x2x4 slice. The times are simulated.
32 devices in a mesh: seq: 4 (over y, x), dp: 8 (over z, core).
Axes of the slice: x: 2, y: 2, z: 4, core: 2. Of those that a mesh axis runs over, the one named last changes fastest.
Arguments:
- tokens_in: bfloat16 [8, 1024, 2560], P('dp', 'seq'), may hold values from -6 to 6
- step_raw: bfloat16 [8, 1024, 40], P('dp', 'seq'), may hold values from -3 to 3
- input_map: bfloat16 [8, 1024, 128], P('dp', 'seq'), may hold values from -1.796875 to 1.796875
- output_map: bfloat16 [8, 1024, 128], P('dp', 'seq'), may hold values from -1.796875 to 1.796875
- decay_log: float32 [40], replicated
- skip_gain: float32 [40], replicated, may hold values from 0.5 to 1.5
- step_bias: float32 [40], replicated, may hold values from -4.7 to -2.2
- grad_out: bfloat16 [8, 1024, 2560], P('dp', 'seq'), may hold values from -6 to 6
Outputs:
- grad_tokens: bfloat16 [8, 1024, 2560], P('dp', 'seq')
- grad_steps: float32 [8, 1024, 40], P('dp', 'seq')
- grad_input_map: float32 [8, 1024, 128], P('dp', 'seq')
- grad_output_map: float32 [8, 1024, 128], P('dp', 'seq')
- grad_decay_log: float32 [40], replicated
- grad_skip_gain: float32 [40], replicated
- grad_step_bias: float32 [40], replicated
All inputs are finite; a program needn't handle non-finite values.
Results may differ from a plain program's by a relative error of at most 0.001.
Values may be sent and summed in bfloat16 or wider, within the bound.
A program may use at most 192 MiB of HBM per device.

v0:
```python
import math

import jax
import jax.numpy as jnp
from jax import lax
from jax.sharding import PartitionSpec as P

SPAN = 256
HEAD_BLOCK = 8


highest = lax.Precision.HIGHEST


def carried_in(shard, axis, combine, identity, reverse):
    size, index = (lax.axis_size(axis), lax.axis_index(axis))
    everything = jax.tree.map(lambda part: lax.all_gather(part, axis), shard)
    start = jax.tree.map(
        lambda part, zero: jnp.broadcast_to(jnp.asarray(zero, part.dtype), part.shape),
        shard,
        identity,
    )

    def turn(k, before):
        at = size - 1 - k if reverse else k
        reached = at > index if reverse else at < index
        new = combine(before, jax.tree.map(lambda part: part[at], everything))
        return jax.tree.map(lambda a, b: jnp.where(reached, a, b), new, before)

    return lax.fori_loop(0, size, turn, start)


def block_forward(head_block, input_rows, output_rows):
    values, step_sizes, decay_rates, skip_part, state_in = head_block
    length = values.shape[0]
    span_count = length // SPAN
    head_count = decay_rates.shape[0]
    head_width = values.shape[2]
    log_decay = -decay_rates[None, :] * step_sizes
    scaled = values * step_sizes[:, :, None]
    causal = lax.broadcasted_iota(jnp.int32, (SPAN, SPAN), 0) >= lax.broadcasted_iota(
        jnp.int32, (SPAN, SPAN), 1
    )

    def advance(state_now, span_item):
        span_in, span_decay, span_b, span_c = span_item
        running = jnp.cumsum(span_decay, axis=0)
        scores = jnp.dot(span_c, span_b.T, precision=highest)
        spread = running.T[:, :, None] - running.T[:, None, :]
        weights = jnp.exp(jnp.where(causal[None], spread, -jnp.inf)) * scores[None]
        inside = jnp.einsum("hts,shp->thp", weights, span_in, precision=highest)
        carried = (
            jnp.einsum("tn,hpn->thp", span_c, state_now, precision=highest)
            * jnp.exp(running)[:, :, None]
        )
        last_sum = running[-1]
        tail_weight = jnp.exp(last_sum[None, :] - running)
        fresh_state = jnp.einsum(
            "shp,sn->hpn", span_in * tail_weight[:, :, None], span_b, precision=highest
        )
        return (jnp.exp(last_sum)[:, None, None] * state_now + fresh_state, inside + carried)

    span_items = (
        scaled.reshape(span_count, SPAN, head_count, head_width),
        log_decay.reshape(span_count, SPAN, head_count),
        input_rows.reshape(span_count, SPAN, -1),
        output_rows.reshape(span_count, SPAN, -1),
    )
    state_out, outputs = lax.scan(advance, state_in, span_items)
    result = outputs.reshape(length, head_count, head_width) + skip_part[None, :, None] * values
    return (result, state_out)


def segment(values, raw_steps, input_rows, output_rows, decay_log, skip_gain, step_bias, state_in):
    length = values.shape[0]
    head_count = decay_log.shape[0]
    head_width = values.shape[1] // head_count
    state_size = input_rows.shape[1]
    per_block = math.gcd(HEAD_BLOCK, head_count)
    blocks = head_count // per_block
    step_sizes = jax.nn.softplus(raw_steps + step_bias[None, :])
    decay_rates = jnp.exp(decay_log)
    packed = (
        values.reshape(length, blocks, per_block, head_width).transpose(1, 0, 2, 3),
        step_sizes.reshape(length, blocks, per_block).transpose(1, 0, 2),
        decay_rates.reshape(blocks, per_block),
        skip_gain.reshape(blocks, per_block),
        state_in.reshape(blocks, per_block, head_width, state_size),
    )
    results, finals = lax.map(
        lambda head_block: block_forward(head_block, input_rows, output_rows), packed
    )
    return (
        results.transpose(1, 0, 2, 3).reshape(length, head_count * head_width),
        finals.reshape(head_count, head_width, state_size),
    )


def link(earlier, later):
    return (earlier[0] * later[0], later[0][:, None] * earlier[1] + later[1])


def on_device(
    tokens_in, step_raw, input_map, output_map, decay_log, skip_gain, step_bias, grad_out
):
    token_rows = tokens_in[0].astype(jnp.float32)
    cotangent = grad_out[0].astype(jnp.float32)
    local_len = token_rows.shape[0]
    head_count = decay_log.shape[0]
    head_width = token_rows.shape[1] // head_count
    state_size = input_map.shape[2]
    seq_count = lax.axis_size("seq")
    group_count = lax.axis_size("dp")
    factor = 1.0 / math.sqrt(group_count * seq_count * local_len * head_width)
    raw_rows = step_raw[0].astype(jnp.float32)
    input_rows = input_map[0].astype(jnp.float32)
    output_rows = output_map[0].astype(jnp.float32)
    step_sizes = jax.nn.softplus(raw_rows + step_bias[None, :])
    log_decay = -jnp.exp(decay_log)[None, :] * step_sizes
    running = jnp.cumsum(log_decay, axis=0)
    total_log = running[-1]
    keep_all = jnp.exp(total_log)
    into_state = jnp.exp(total_log[None, :] - running) * step_sizes
    weighted_in = (
        token_rows.reshape(local_len, head_count, head_width) * into_state[:, :, None]
    ).reshape(local_len, -1)
    local_state = jnp.einsum("tk,tn->kn", weighted_in, input_rows, precision=highest).reshape(
        head_count, head_width * state_size
    )
    weighted_out = (
        cotangent.reshape(local_len, head_count, head_width) * jnp.exp(running)[:, :, None]
    ).reshape(local_len, -1)
    local_grad = jnp.einsum("tk,tn->kn", weighted_out, output_rows, precision=highest).reshape(
        head_count, head_width * state_size
    )
    identity = (
        jnp.ones((head_count,), jnp.float32),
        jnp.zeros((head_count, head_width * state_size), jnp.float32),
    )
    entering = carried_in((keep_all, local_state), "seq", link, identity, False)[1]
    leaving = carried_in((keep_all, local_grad), "seq", link, identity, True)[1]
    start_state = entering.reshape(head_count, head_width, state_size)
    output, pullback = jax.vjp(
        lambda primals: segment(*primals, start_state),
        (token_rows, raw_rows, input_rows, output_rows, decay_log, skip_gain, step_bias),
    )
    gradients = pullback((cotangent, leaving.reshape(head_count, head_width, state_size)))[0]
    grad_tokens = gradients[0].astype(jnp.bfloat16)
    grad_steps = gradients[1]
    grad_first = gradients[2]
    grad_second = gradients[3]
    grad_rates = gradients[4]
    grad_skip = gradients[5]
    grad_bias = gradients[6]
    rate_total, skip_result, bias_total = lax.psum(
        (grad_rates, grad_skip, grad_bias), ("seq", "dp")
    )
    return (
        grad_tokens[None],
        grad_steps[None],
        grad_first[None],
        grad_second[None],
        rate_total * factor,
        skip_result * factor,
        bias_total * factor,
    )


def solution(mesh):
    in_specs = (
        P("dp", "seq", None),
        P("dp", "seq", None),
        P("dp", "seq", None),
        P("dp", "seq", None),
        P(),
        P(),
        P(),
        P("dp", "seq", None),
    )
    out_specs = (
        P("dp", "seq", None),
        P("dp", "seq", None),
        P("dp", "seq", None),
        P("dp", "seq", None),
        P(),
        P(),
        P(),
    )
    return jax.shard_map(
        on_device, mesh=mesh, in_specs=in_specs, out_specs=out_specs, check_vma=False
    )
```

profile of v0, /device:TPU:0, one launch (start us, length us, event | category | flops | bytes accessed | tf_op | source)
XLA Modules:
  0.0 420.2 jit_solution(15115620566088745981)
XLA Ops:
  14.8 3.4 broadcast_multiply_fusion.1
  30.7 9.6 %all-gather = f32[4,1,40]{2,1,0:T(1,128)S(1)} all-gather(f32[1,1,40]{2,1,0:T(1,128)S(1)} %bitcast.500), channel_id=1, replica_groups=mesh['seq'=4,'dp'=8] {'seq'}, dimensions={0}, use_global_device_ids=true | all-gather | bytes 800 | tf_op jit(solution)/shard_map/all_gather | solution.py:17
  41.8 45.6 %all-gather.4.cloned.1.call-done = f32[4,40,8192]{2,1,0:T(8,128)} async-done(((f32[1,40,8192]{2,1,0:T(8,128)}), f32[4,40,8192]{2,1,0:T(8,128)}) %all-gather.4.cloned.1.call-update) | async-done | bytes 5242896 | tf_op jit(solution)/shard_map/all_gather | solution.py:17
  87.4 12.0 %while.84 = (s32[]{:T(128)}, f32[40,8192]{1,0:T(8,128)}, s32[]{:T(128)}, f32[4,40]{1,0:T(4,128)S(1)}, f32[4,40,8192]{2,1,0:T(8,128)}, /*index=5*/s32[]{:T(128)}, s32[]{:T(128)}) while((s32[]{:T(128)}, f32[40,8192]{1,0:T(8,128)}, s32[]{:T(128)}, f32[4,40]{1,0:T(4,128)S(1)}, f32[4,40,8192]{2,1,0:T(8,128)}, /*index=5*/s32[]{:T(128)}, ...), condition=%wide.region_5.6_spmd.clone, body=%wide.region_4.5_spmd.clone.sunk | while | flops 1310724 | bytes 3932745 | solution.py:30
  87.4 2.6 fusion.142
  90.0 3.0 fusion.142
  93.0 3.0 fusion.142
  96.0 3.4 fusion.142
  99.9 90.5 %while.83 = (s32[]{:T(128)}, f32[5,1,8]{2,1,0:T(1,128)}, f32[5,256,8,1]{1,2,3,0:T(8,128)}, f32[5,1,8,256,256]{4,3,2,1,0:T(8,128)}, f32[5,1,8,256,256]{4,3,2,1,0:...) while((s32[]{:T(128)}, f32[5,1,8]{2,1,0:T(1,128)}, ...), condition=%wide.region_9.10_spmd.clone, body=%wide.region_6.9_spmd.clone.sunk | while | flops 203429936 | bytes 16680513 | solution.py:90
  101.6 3.3 multiply_dynamic-update-slice_fusion.2
  119.6 3.4 multiply_dynamic-update-slice_fusion.2
  137.7 3.3 multiply_dynamic-update-slice_fusion.2
  155.8 3.4 multiply_dynamic-update-slice_fusion.2
  174.0 3.4 multiply_dynamic-update-slice_fusion.2
  191.2 14.3 %while.85 = (s32[]{:T(128)}, f32[40,8192]{1,0:T(8,128)}, s32[]{:T(128)}, f32[4,40]{1,0:T(4,128)}, f32[4,40,8192]{2,1,0:T(8,128)}, /*index=5*/s32[]{:T(128)}, s32[]{:T(128)}, s32[]{:T(128)}, s32[]{:T(128)}) while((s32[]{:T(128)}, f32[40,8192]{1,0:T(8,128)}, s32[]{:T(128)}, f32[4,40]{1,0:T(4,128)}, f32[4,40,8192]{2,1,0:T(8,128)}, ...), condition=%wide.region_3.4_spmd.clone, body=%wide.region_2.3_spmd.clone.sunk | while | flops 1310728 | bytes 3932807 | solution.py:30
  191.9 2.6 fusion.143
  195.1 3.0 fusion.143
  198.8 3.0 fusion.143
  202.5 3.0 fusion.143
  205.5 2.8 copy.108
  210.7 155.2 %while.86 = (s32[]{:T(128)}, f32[256,128]{1,0:T(8,128)}, f32[256,128]{1,0:T(8,128)}, bf16[5,256,8,64]{1,3,2,0:T(8,128)(2,1)}, f32[5,256,8]{1,2,0:T(8,128)}, /*in...) while((s32[]{:T(128)}, f32[256,128]{1,0:T(8,128)}, ...), condition=%wide.region_23.24_spmd.clone, body=%wide.region_10.23_spmd.clone.sunk | while | flops 1616662528 | bytes 16179480 | solution.py:90
  214.7 3.8 bitcast_dynamic-update-slice_fusion.18
  222.9 4.2 fusion.152
  245.1 3.8 bitcast_dynamic-update-slice_fusion.18
  253.1 4.2 fusion.152
  276.3 3.8 bitcast_dynamic-update-slice_fusion.18
  284.3 4.2 fusion.152
  307.4 3.8 bitcast_dynamic-update-slice_fusion.18
  315.5 4.2 fusion.152
  338.6 3.7 bitcast_dynamic-update-slice_fusion.18
  346.6 4.2 fusion.152
  370.0 39.3 %all-reduce.1 = (f32[40]{0:T(128)S(1)}, f32[40]{0:T(128)S(1)}, f32[40]{0:T(128)S(1)}) all-reduce(f32[40]{0:T(128)S(1)} %exponential_multiply_fusion.1, f32[40]{0:T(128)S(1)} %reshape.481, f32[40]{0:T(128)S(1)} %reduce_sum.234), channel_id=1, replica_groups=mesh['seq'=4,'dp'=8] {'seq','dp'}, use_global_device_ids=true, to_apply=%region_24.25 | all-reduce | flops 120 | bytes 960 | tf_op jit(solution)/shard_map/psum | solution.py:155
  (410 shorter events, 224.4 us)
Async XLA Ops:
  7.2 80.2 %all-gather.4.cloned.1.call-start = ((), (), s32[]{:S(2)}) async-start(), calls=%async_computation | async-start | bytes 6553600 | tf_op jit(solution)/shard_map/all_gather | solution.py:17
  14.8 3.4 copy-start
  14.8 3.4 copy-start.9
  20.6 2.6 copy-start.8
  23.2 167.3 %all-gather.6.cloned.1.call-start = ((), (), s32[]{:S(2)}) async-start(), calls=%async_computation.1 | async-start | bytes 6553600 | tf_op jit(solution)/shard_map/all_gather | solution.py:17
  25.6 2.6 copy-start.16
  25.6 14.7 %copy-start.10 = (bf16[1,256,40]{1,2,0:T(8,128)(2,1)S(1)}, bf16[1,256,40]{1,2,0:T(8,128)(2,1)}, u32[]{:S(2)}) copy-start(bf16[1,256,40]{1,2,0:T(8,128)(2,1)} %param.17) | copy-start | bytes 61444
  25.6 15.5 %copy-start.18 = (f32[40]{0:T(128)S(1)}, f32[40]{0:T(128)}, u32[]{:S(2)}) copy-start(f32[40]{0:T(128)} %param.21) | copy-start | bytes 484
  28.3 59.1 %copy-start.12 = (f32[5,8]{1,0:T(8,128)}, f32[5,8]{1,0:T(8,128)S(1)}, u32[]{:S(2)}) copy-start(f32[5,8]{1,0:T(8,128)S(1)} %add.149) | copy-start | bytes 484
  99.9 5.0 %copy-start.2 = (f32[1,1,256,256]{3,2,1,0:T(8,128)}, f32[1,1,256,256]{3,2,1,0:T(8,128)S(1)}, u32[]{:S(2)}) copy-start(f32[1,1,256,256]{3,2,1,0:T(8,128)S(1)} %get-tuple-element.2435) | copy-start | bytes 786436 | tf_op jit(solution)/shard_map/jvp()/while
  99.9 5.0 %copy-start.14 = (f32[5,8]{1,0:T(8,128)}, f32[5,8]{1,0:T(8,128)S(1)}, u32[]{:S(2)}) copy-start(f32[5,8]{1,0:T(8,128)S(1)} %get-tuple-element.2433) | copy-start | bytes 484 | tf_op jit(solution)/shard_map/jvp()/while
  110.1 7.8 %copy-start.3 = (f32[1,1,256,256]{3,2,1,0:T(8,128)S(1)}, f32[1,1,256,256]{3,2,1,0:T(8,128)}, u32[]{:S(2)}) copy-start(f32[1,1,256,256]{3,2,1,0:T(8,128)} %copy-done.2) | copy-start | bytes 786436 | tf_op jit(solution)/shard_map/jvp()/while
  117.9 5.0 %copy-start.2 = (f32[1,1,256,256]{3,2,1,0:T(8,128)}, f32[1,1,256,256]{3,2,1,0:T(8,128)S(1)}, u32[]{:S(2)}) copy-start(f32[1,1,256,256]{3,2,1,0:T(8,128)S(1)} %get-tuple-element.2435) | copy-start | bytes 786436 | tf_op jit(solution)/shard_map/jvp()/while
  117.9 5.0 %copy-start.14 = (f32[5,8]{1,0:T(8,128)}, f32[5,8]{1,0:T(8,128)S(1)}, u32[]{:S(2)}) copy-start(f32[5,8]{1,0:T(8,128)S(1)} %get-tuple-element.2433) | copy-start | bytes 484 | tf_op jit(solution)/shard_map/jvp()/while
  128.2 7.9 %copy-start.3 = (f32[1,1,256,256]{3,2,1,0:T(8,128)S(1)}, f32[1,1,256,256]{3,2,1,0:T(8,128)}, u32[]{:S(2)}) copy-start(f32[1,1,256,256]{3,2,1,0:T(8,128)} %copy-done.2) | copy-start | bytes 786436 | tf_op jit(solution)/shard_map/jvp()/while
  136.1 5.0 %copy-start.2 = (f32[1,1,256,256]{3,2,1,0:T(8,128)}, f32[1,1,256,256]{3,2,1,0:T(8,128)S(1)}, u32[]{:S(2)}) copy-start(f32[1,1,256,256]{3,2,1,0:T(8,128)S(1)} %get-tuple-element.2435) | copy-start | bytes 786436 | tf_op jit(solution)/shard_map/jvp()/while
  136.1 5.0 %copy-start.14 = (f32[5,8]{1,0:T(8,128)}, f32[5,8]{1,0:T(8,128)S(1)}, u32[]{:S(2)}) copy-start(f32[5,8]{1,0:T(8,128)S(1)} %get-tuple-element.2433) | copy-start | bytes 484 | tf_op jit(solution)/shard_map/jvp()/while
  145.8 2.1 copy-start.11
  145.9 2.1 copy-start.15
  146.2 7.9 %copy-start.3 = (f32[1,1,256,256]{3,2,1,0:T(8,128)S(1)}, f32[1,1,256,256]{3,2,1,0:T(8,128)}, u32[]{:S(2)}) copy-start(f32[1,1,256,256]{3,2,1,0:T(8,128)} %copy-done.2) | copy-start | bytes 786436 | tf_op jit(solution)/shard_map/jvp()/while
  154.1 5.0 %copy-start.2 = (f32[1,1,256,256]{3,2,1,0:T(8,128)}, f32[1,1,256,256]{3,2,1,0:T(8,128)S(1)}, u32[]{:S(2)}) copy-start(f32[1,1,256,256]{3,2,1,0:T(8,128)S(1)} %get-tuple-element.2435) | copy-start | bytes 786436 | tf_op jit(solution)/shard_map/jvp()/while
  154.1 5.0 %copy-start.14 = (f32[5,8]{1,0:T(8,128)}, f32[5,8]{1,0:T(8,128)S(1)}, u32[]{:S(2)}) copy-start(f32[5,8]{1,0:T(8,128)S(1)} %get-tuple-element.2433) | copy-start | bytes 484 | tf_op jit(solution)/shard_map/jvp()/while
  164.0 2.1 copy-start.11
  164.0 2.1 copy-start.15
  164.4 7.9 %copy-start.3 = (f32[1,1,256,256]{3,2,1,0:T(8,128)S(1)}, f32[1,1,256,256]{3,2,1,0:T(8,128)}, u32[]{:S(2)}) copy-start(f32[1,1,256,256]{3,2,1,0:T(8,128)} %copy-done.2) | copy-start | bytes 786436 | tf_op jit(solution)/shard_map/jvp()/while
  172.3 5.0 %copy-start.2 = (f32[1,1,256,256]{3,2,1,0:T(8,128)}, f32[1,1,256,256]{3,2,1,0:T(8,128)S(1)}, u32[]{:S(2)}) copy-start(f32[1,1,256,256]{3,2,1,0:T(8,128)S(1)} %get-tuple-element.2435) | copy-start | bytes 786436 | tf_op jit(solution)/shard_map/jvp()/while
  172.3 5.0 %copy-start.14 = (f32[5,8]{1,0:T(8,128)}, f32[5,8]{1,0:T(8,128)S(1)}, u32[]{:S(2)}) copy-start(f32[5,8]{1,0:T(8,128)S(1)} %get-tuple-element.2433) | copy-start | bytes 484 | tf_op jit(solution)/shard_map/jvp()/while
  182.5 7.9 %copy-start.3 = (f32[1,1,256,256]{3,2,1,0:T(8,128)S(1)}, f32[1,1,256,256]{3,2,1,0:T(8,128)}, u32[]{:S(2)}) copy-start(f32[1,1,256,256]{3,2,1,0:T(8,128)} %copy-done.2) | copy-start | bytes 786436 | tf_op jit(solution)/shard_map/jvp()/while
  205.5 5.2 %copy-start.1 = (f32[1,256,2560]{1,2,0:T(8,128)S(1)}, f32[1,256,2560]{1,2,0:T(8,128)}, u32[]{:S(2)}) copy-start(f32[1,256,2560]{1,2,0:T(8,128)} %copy-done) | copy-start | bytes 7864324
  205.5 5.2 %copy-start.5 = (f32[1,1,256,256]{3,2,1,0:T(8,128)S(1)}, f32[1,1,256,256]{3,2,1,0:T(8,128)}, u32[]{:S(2)}) copy-start(f32[1,1,256,256]{3,2,1,0:T(8,128)} %copy-done.4) | copy-start | bytes 786436
  205.5 5.2 %copy-start.6 = (f32[1,256,128]{2,1,0:T(8,128)S(1)}, f32[1,256,128]{2,1,0:T(8,128)}, u32[]{:S(2)}) copy-start(f32[1,256,128]{2,1,0:T(8,128)} %copy.82) | copy-start | bytes 393220
  210.7 155.2 %copy-start.13 = (f32[5,8]{1,0:T(8,128)S(1)}, f32[5,8]{1,0:T(8,128)}, u32[]{:S(2)}) copy-start(f32[5,8]{1,0:T(8,128)} %copy-done.12) | copy-start | bytes 484
  (9 other events, 15.5 us)
Sparse Core Ops, SparseCore 0:
  23.3 64.0 all-gather.3
  89.2 61.3 all-gather.5
where the time goes:
time: 425 us; the launch traced here: 420 us
  other arithmetic  117 us (28%)
  matrix products  100 us (24%)
  local copies, waits for them, and re-layouts  93.2 us (22%)
  blocking collectives  48.9 us (12%)
  waiting for transfers between devices  45.7 us (11%)
  between operations  14.3 us (3%)
    all_gather x2, waiting for transfers between devices, carried_in(): everything = jax.tree.map(lambda part: lax.all_gather(part, axis), shard)  45.6 us
    dot_general x10, matrix products, advance(): inside = jnp.einsum('hts,shp->thp', weights, span_in, precision=highest)  39.7 us
    psum x1, blocking collectives, on_device(): lax.psum((grad_rates, grad_skip, grad_bias), ('seq', 'dp'))  39.3 us
    dynamic_update_slice x45, local copies, waits for them, and re-layouts, segment(): lax.map(lambda head_block: block_forward(head_block, input_rows, output_r...  35.1 us
    dynamic_update_slice x25, other arithmetic, segment(): lax.map(lambda head_block: block_forward(head_block, input_rows, output_r...  29.4 us
    another operation x50, other arithmetic  25.7 us
    select_n x8, other arithmetic, turn(): return jax.tree.map(lambda a, b: jnp.where(reached, a, b), new, before)  23.6 us
    dot_general x11, matrix products, advance(): scores = jnp.dot(span_c, span_b.T, precision=highest)  20.1 us
  transfers between devices with their start and end apart: 2, of which 1 were waited for; matrix products, arithmetic and copies ran while one was open for 26% of the time, Pallas kernels for 0%

commit v1 on v0

v1 whole, which is shorter than its diff:
```python
import functools
import math

import jax
import jax.numpy as jnp
from jax import lax
from jax.experimental import pallas as pl
from jax.experimental.pallas import tpu as pltpu
from jax.sharding import PartitionSpec as P

F32 = jnp.float32
BF16 = jnp.bfloat16
LANES = 128
EXTRA = 8
WIRE = jnp.float32


def dot(a, b, dims=((1,), (0,))):
    return lax.dot_general(a, b, (dims, ((), ())), preferred_element_type=F32)


def split2(v):
    hi = v.astype(BF16)
    return hi, (v - hi.astype(F32)).astype(BF16)


def split3(v):
    hi = v.astype(BF16)
    rest = v - hi.astype(F32)
    mid = rest.astype(BF16)
    return hi, mid, (rest - mid.astype(F32)).astype(BF16)


def exact_sum(mask, v):
    a, b, c = split3(v)
    return dot(mask, a) + (dot(mask, b) + dot(mask, c))


def expand(columns, first, count, width):
    rows = columns.shape[0]
    per = LANES // width
    lane = lax.broadcasted_iota(jnp.int32, (rows, LANES), 1)
    out = []
    for j in range(0, count, per):
        value = jnp.broadcast_to(columns[:, first + j : first + j + 1], (rows, LANES))
        for k in range(1, per):
            more = jnp.broadcast_to(columns[:, first + j + k : first + j + k + 1], (rows, LANES))
            value = jnp.where(lane < k * width, value, more)
        out.append(value)
    return jnp.concatenate(out, axis=1)


def turn(columns, by):
    return pltpu.roll(columns, lax.rem(LANES - by, LANES), 1)


def state_kernel(
    n, per, width, me_ref, raw_ref, bias_ref, rate_ref, b_ref, c_ref, x_ref, g_ref, *refs
):
    sends = refs[: n - 1]
    dt_ref, run_ref, run_t_ref, sig_ref, into_ref, grow_ref, scr, bt_ref, ct_ref = refs[n - 1 :]
    step = pl.program_id(0)
    heads = raw_ref.shape[1]
    length = raw_ref.shape[0]

    @pl.when(step == 0)
    def _():
        scr[...] = jnp.zeros_like(scr)
        scr[:, :heads] = raw_ref[...].astype(F32) + bias_ref[...]
        value = scr[...]
        dt = jnp.maximum(value, 0.0) + jnp.log1p(jnp.exp(-jnp.abs(value)))
        dt_ref[...] = dt
        sig_ref[...] = 1.0 / (1.0 + jnp.exp(-value))
        scr[0:1, :heads] = jnp.exp(rate_ref[...])
        decay = -scr[0:1, :] * dt
        row = lax.broadcasted_iota(jnp.int32, (length, length), 0)
        col = lax.broadcasted_iota(jnp.int32, (length, length), 1)
        lower = jnp.where(row >= col, 1.0, 0.0).astype(BF16)
        running = exact_sum(lower, decay)
        run_ref[...] = running
        run_t_ref[...] = running.T
        into_ref[...] = jnp.exp(running[length - 1 : length] - running) * dt
        grow_ref[...] = jnp.exp(running)
        bt_ref[...] = b_ref[...].astype(F32).T.astype(BF16)
        ct_ref[...] = c_ref[...].astype(F32).T.astype(BF16)

    me = me_ref[0]
    first = step * per
    into = turn(into_ref[...], first)
    grow = turn(grow_ref[...], first)
    last = turn(run_ref[length - EXTRA : length, :], first)
    xw = x_ref[...].astype(F32) * expand(into, 0, per, width)
    gw = g_ref[...].astype(F32) * expand(grow, 0, per, width)
    x_hi, x_lo = split2(xw)
    g_hi, g_lo = split2(gw)
    states = bt_ref.shape[0]
    state = dot(bt_ref[...], x_hi) + dot(bt_ref[...], x_lo)
    grad = dot(ct_ref[...], g_hi) + dot(ct_ref[...], g_lo)
    extra = expand(last, 0, per, width)
    for k in range(1, n):
        sends[k - 1][:states, :] = jnp.where(me + k < n, state, grad).astype(WIRE)
        sends[k - 1][states:, :] = extra.astype(WIRE)


def inside_kernel(
    per, width, run_ref, run_t_ref, dt_ref, b_ref, c_ref, x_ref, g_ref,
    gx_ref, rows_ref, db_ref, dc_ref, cb_ref, acc_ref,
):
    step = pl.program_id(0)
    length = run_ref.shape[0]
    tile = LANES
    nt = ((1,), (1,))

    @pl.when(step == 0)
    def _():
        cb_ref[...] = dot(b_ref[...], c_ref[...], nt)
        acc_ref[...] = jnp.zeros_like(acc_ref)

    run = turn(run_ref[...], step * per)
    dt = turn(dt_ref[...], step * per)
    group = LANES // width
    lane = lax.broadcasted_iota(jnp.int32, (1, LANES), 1)
    causal = lax.broadcasted_iota(jnp.int32, (tile, tile), 0) <= lax.broadcasted_iota(
        jnp.int32, (tile, tile), 1
    )
    for pair in range(per // group):
        x_pair = x_ref[:, pair * LANES : (pair + 1) * LANES]
        g_pair = g_ref[:, pair * LANES : (pair + 1) * LANES]
        zero = jnp.zeros_like(g_pair)
        totals = [None] * (length // tile)
        for k in range(group):
            head = pair * group + k
            own = (lane >= k * width) & (lane < (k + 1) * width)
            g_own = jnp.where(own, g_pair, zero)
            column_sums = [None] * (length // tile)
            for sb in range(length // tile):
                rows = slice(sb * tile, (sb + 1) * tile)
                t0 = sb * tile
                dw = dot(x_pair[rows], g_own[t0:], nt)
                run_s = jnp.broadcast_to(run[rows, head : head + 1], (tile, tile))
                dt_s = jnp.broadcast_to(dt[rows, head : head + 1], (tile, tile))
                parts_hi, parts_lo = [], []
                for tb in range(sb, length // tile):
                    cols = slice(tb * tile, (tb + 1) * tile)
                    spread = run_t_ref[head : head + 1, cols] - run_s
                    if tb == sb:
                        spread = jnp.where(causal, spread, -jnp.inf)
                    q = jnp.exp(spread) * dt_s
                    dw_t = dw[:, tb * tile - t0 : (tb + 1) * tile - t0]
                    w = q * cb_ref[rows, cols]
                    acc_ref[rows, cols] += q * dw_t
                    part = jnp.sum(w * dw_t, axis=0, keepdims=True)
                    column_sums[tb] = part if column_sums[tb] is None else column_sums[tb] + part
                    hi, lo = split2(w)
                    parts_hi.append(hi)
                    parts_lo.append(lo)
                w_hi = jnp.concatenate(parts_hi, axis=1)
                w_lo = jnp.concatenate(parts_lo, axis=1)
                out = dot(w_hi, g_own[t0:]) + dot(w_lo, g_own[t0:])
                totals[sb] = out if totals[sb] is None else totals[sb] + out
            for tb in range(length // tile):
                rows_ref[head : head + 1, tb * tile : (tb + 1) * tile] = column_sums[tb]
        for sb in range(length // tile):
            gx_ref[sb * tile : (sb + 1) * tile, pair * LANES : (pair + 1) * LANES] = totals[sb]

    @pl.when(step == pl.num_programs(0) - 1)
    def _():
        acc = acc_ref[...]
        hi, lo = split2(acc)
        db_ref[...] = dot(hi, c_ref[...]) + dot(lo, c_ref[...])
        hi_t, lo_t = split2(acc.T)
        dc_ref[...] = dot(hi_t, b_ref[...]) + dot(lo_t, b_ref[...])


def carried_kernel(
    n, per, width, me_ref, skip_ref, rate_ref, run_ref, dt_ref, sig_ref, into_ref, grow_ref,
    b_ref, c_ref, inner_ref, db_in_ref, dc_in_ref, x_ref, g_ref, gx_ref, *refs
):
    arrived = refs[: n - 1]
    tokens_ref, steps_ref, db_ref, dc_ref, param_ref = refs[n - 1 : n + 4]
    direct_ref, carry_ref, small_ref, pad_ref = refs[n + 4 :]
    step = pl.program_id(0)
    length = run_ref.shape[0]
    states = b_ref.shape[1]
    heads = steps_ref.shape[1]
    span = x_ref.shape[1]
    nt = ((1,), (1,))
    me = me_ref[0]
    first = step * per

    @pl.when(step == 0)
    def _():
        db_ref[...] = db_in_ref[...]
        dc_ref[...] = dc_in_ref[...]
        direct_ref[...] = jnp.zeros_like(direct_ref)
        carry_ref[...] = jnp.zeros_like(carry_ref)
        small_ref[...] = jnp.zeros_like(small_ref)
        pad_ref[...] = jnp.zeros_like(pad_ref)

    def gather(order, limit):
        total = jnp.zeros((states, span), F32)
        passed = jnp.zeros((1, span), F32)
        for j, slot in enumerate(order):
            take = jnp.where(j + 1 <= limit, 1.0, 0.0)
            block = arrived[slot]
            total = total + (take * jnp.exp(passed)) * block[:states, :].astype(F32)
            low = block[states : states + EXTRA, :].astype(F32)[EXTRA - 1 : EXTRA]
            passed = passed + jnp.where(j + 1 <= limit, low, 0.0)
        return total

    entering = gather([k - 1 for k in range(1, n)], me)
    leaving = gather([n - j - 1 for j in range(1, n)], n - 1 - me)
    s_hi, s_lo = split2(entering)
    g_hi, g_lo = split2(leaving)
    grow = expand(turn(grow_ref[...], first), 0, per, width)
    into = expand(turn(into_ref[...], first), 0, per, width)
    x = x_ref[...].astype(F32)
    g = g_ref[...].astype(F32)
    gxc = into * (dot(b_ref[...], g_hi) + dot(b_ref[...], g_lo))
    yc = dot(c_ref[...], s_hi) + dot(c_ref[...], s_lo)
    gx = gx_ref[...] + gxc
    lane_head = lax.broadcasted_iota(jnp.int32, (1, span), 1) // width
    gain = jnp.zeros((1, span), F32)
    for j in range(per):
        gain = jnp.where(lane_head == j, skip_ref[first + j], gain)
    tokens_ref[...] = (gx + gain * g).astype(BF16)
    gw = grow * g
    a_hi, a_lo = split2(gw)
    dc_ref[...] += dot(a_hi, s_hi, nt) + (dot(a_lo, s_hi, nt) + dot(a_hi, s_lo, nt))
    b_hi, b_lo = split2(into * x)
    db_ref[...] += dot(b_hi, g_hi, nt) + (dot(b_lo, g_hi, nt) + dot(b_hi, g_lo, nt))
    pick = (
        first + lax.broadcasted_iota(jnp.int32, (span, LANES), 0) // width
        == lax.broadcasted_iota(jnp.int32, (span, LANES), 1)
    )
    pick = jnp.where(pick, 1.0, 0.0).astype(BF16)
    d_hi, d_lo = split2(x * gx)
    direct_ref[...] += dot(d_hi, pick) + dot(d_lo, pick)
    e_hi, e_lo = split2(gw * yc)
    carry_ref[...] += dot(e_hi, pick) + dot(e_lo, pick)
    keep = grow[length - 1 : length]
    at_end = jnp.sum(x * gxc, axis=0, keepdims=True) + keep * jnp.sum(
        entering * leaving, axis=0, keepdims=True
    )
    both = jnp.sum(x * g, axis=0, keepdims=True)
    row = lax.broadcasted_iota(jnp.int32, (EXTRA, span), 0)
    packed = jnp.where(row == 0, at_end, jnp.where(row == 1, both, 0.0))
    p1, p2, p3 = split3(packed)
    small_ref[...] += dot(p1, pick) + (dot(p2, pick) + dot(p3, pick))

    @pl.when(step == pl.num_programs(0) - 1)
    def _():
        pad_ref[:heads, :] = inner_ref[...]
        direct = direct_ref[...]
        grad_run = pad_ref[...].T + carry_ref[...] - direct
        small = small_ref[...]
        at = lax.broadcasted_iota(jnp.int32, (length, LANES), 0)
        grad_run = grad_run + jnp.where(at == length - 1, small[0:1], 0.0)
        r = lax.broadcasted_iota(jnp.int32, (length, length), 0)
        c = lax.broadcasted_iota(jnp.int32, (length, length), 1)
        upper = jnp.where(r <= c, 1.0, 0.0).astype(BF16)
        grad_decay = exact_sum(upper, grad_run)
        dt = dt_ref[...]
        pad_ref[0:1, :LANES] = jnp.ones((1, LANES), F32)
        pad_ref[0:1, :heads] = jnp.exp(rate_ref[...])
        rate = pad_ref[0:1, :LANES]
        grad_raw = (direct / dt - rate * grad_decay) * sig_ref[...]
        steps_ref[...] = grad_raw[:, :heads]
        rates = jnp.sum(-rate * dt * grad_decay, axis=0, keepdims=True)
        bias = jnp.sum(grad_raw, axis=0, keepdims=True)
        line = lax.broadcasted_iota(jnp.int32, (EXTRA, LANES), 0)
        param_ref[...] = jnp.where(
            line == 0, rates, jnp.where(line == 1, small[1:2], jnp.where(line == 2, bias, 0.0))
        )


def whole(shape):
    return pl.BlockSpec(shape, lambda i: tuple(0 for _ in shape))


def on_device(
    tokens_in, step_raw, input_map, output_map, decay_log, skip_gain, step_bias, grad_out
):
    x, raw, b, c, g = tokens_in[0], step_raw[0], input_map[0], output_map[0], grad_out[0]
    length, channels = x.shape
    heads = decay_log.shape[0]
    width = channels // heads
    states = b.shape[1]
    n = lax.axis_size("seq")
    groups = lax.axis_size("dp")
    factor = 1.0 / math.sqrt(groups * n * length * width)
    per = math.gcd(8, heads)
    span = per * width
    grid = (heads // per,)
    me = lax.axis_index("seq").astype(jnp.int32)[None]
    smem = pl.BlockSpec(memory_space=pltpu.SMEM)
    scalars = jax.ShapeDtypeStruct((length, LANES), F32)
    cols = pl.BlockSpec((length, span), lambda i: (0, i))
    tall = states + EXTRA
    message = pl.BlockSpec((tall, span), lambda i: (0, i))
    rows = [whole((length, LANES))]
    rate_row, bias_row = decay_log[None], step_bias[None]

    def cost(flops, transfer):
        return pl.CostEstimate(flops=flops, bytes_accessed=transfer, transcendentals=0)

    params = pltpu.CompilerParams(dimension_semantics=("arbitrary",))
    made = pl.pallas_call(
        functools.partial(state_kernel, n, per, width),
        grid=grid,
        in_specs=[smem, whole((length, heads)), whole((1, heads)), whole((1, heads)),
                  whole((length, states)), whole((length, states)), cols, cols],
        out_specs=[message] * (n - 1) + rows * 2 + [whole((LANES, length))] + rows * 3,
        out_shape=[jax.ShapeDtypeStruct((tall, channels), WIRE)] * (n - 1)
        + [scalars, scalars, jax.ShapeDtypeStruct((LANES, length), F32)] + [scalars] * 3,
        scratch_shapes=[pltpu.VMEM((length, LANES), F32), pltpu.VMEM((states, length), BF16),
                        pltpu.VMEM((states, length), BF16)],
        compiler_params=params,
        name="states",
    )(me, raw, bias_row, rate_row, b, c, x, g)
    sends = made[: n - 1]
    dt, run, run_t, sig, into, grow = made[n - 1 :]
    arrived = [
        lax.ppermute(sends[k - 1], "seq", [(d, (d + k) % n) for d in range(n)])
        for k in range(1, n)
    ]
    gx, inner, db_in, dc_in = pl.pallas_call(
        functools.partial(inside_kernel, per, width),
        grid=grid,
        in_specs=[whole((length, LANES)), pl.BlockSpec((per, length), lambda i: (i, 0)),
                  whole((length, LANES)),
                  whole((length, states)), whole((length, states)), cols, cols],
        out_specs=[cols, pl.BlockSpec((per, length), lambda i: (i, 0)),
                   whole((length, states)), whole((length, states))],
        out_shape=[jax.ShapeDtypeStruct((length, channels), F32),
                   jax.ShapeDtypeStruct((heads, length), F32),
                   jax.ShapeDtypeStruct((length, states), F32),
                   jax.ShapeDtypeStruct((length, states), F32)],
        scratch_shapes=[pltpu.VMEM((length, length), F32), pltpu.VMEM((length, length), F32)],
        compiler_params=params,
        cost_estimate=cost(10**10, 10**7),
        name="inside",
    )(run, run_t, dt, b, c, x, g)
    grad_tokens, grad_steps, db, dc, param = pl.pallas_call(
        functools.partial(carried_kernel, n, per, width),
        grid=grid,
        in_specs=[smem, smem, whole((1, heads))] + rows * 5
        + [whole((length, states)), whole((length, states)), whole((heads, length)),
           whole((length, states)), whole((length, states)), cols, cols, cols]
        + [message] * (n - 1),
        out_specs=[cols, whole((length, heads)), whole((length, states)),
                   whole((length, states)), whole((EXTRA, LANES))],
        out_shape=[jax.ShapeDtypeStruct((length, channels), BF16),
                   jax.ShapeDtypeStruct((length, heads), F32),
                   jax.ShapeDtypeStruct((length, states), F32),
                   jax.ShapeDtypeStruct((length, states), F32),
                   jax.ShapeDtypeStruct((EXTRA, LANES), F32)],
        scratch_shapes=[pltpu.VMEM((length, LANES), F32), pltpu.VMEM((length, LANES), F32),
                        pltpu.VMEM((EXTRA, LANES), F32), pltpu.VMEM((LANES, length), F32)],
        compiler_params=params,
        name="carried",
    )(me, skip_gain, rate_row, run, dt, sig, into, grow, b, c, inner, db_in, dc_in, x, g, gx,
      *arrived)
    total = lax.psum(param, ("seq", "dp")) * factor
    return (
        grad_tokens[None],
        grad_steps[None],
        db[None],
        dc[None],
        total[0, :heads],
        total[1, :heads],
        total[2, :heads],
    )


def solution(mesh):
    wide = P("dp", "seq", None)
    return jax.shard_map(
        on_device,
        mesh=mesh,
        in_specs=(wide, wide, wide, wide, P(), P(), P(), wide),
        out_specs=(wide, wide, wide, wide, P(), P(), P()),
        check_vma=False,
    )
```

time: 425 us -> 131 us (0.31); the launches traced: 420 us -> 130 us
  other arithmetic: 117 us -> 0.01 us
  matrix products: 100 us -> 0 us
  local copies, waits for them, and re-layouts: 93.2 us -> 4.28 us
  Pallas kernels: 0 us -> 29.4 us
  between operations: 14.3 us -> 0.65 us
  blocking collectives: 48.9 us -> 40.2 us
  starting transfers between devices: 0.08 us -> 5.94 us
  waiting for transfers between devices: 45.7 us -> 50 us
    dot_general x43 -> x0, matrix products: 100 us -> none  [the longest x10 39.7 us: advance(): inside = jnp.einsum('hts,shp->thp', weights, span_in, precision=highest)]
    ppermute x0 -> x3, waiting for transfers between devices: none -> 50 us  [on_device(): lax.ppermute(sends[k - 1], 'seq', [(d, (d + k) % n) for d in range(n)])]
    all_gather x2 -> x0, waiting for transfers between devices: 45.6 us -> none  [carried_in(): everything = jax.tree.map(lambda part: lax.all_gather(part, axis), shard)]
    dynamic_update_slice x45 -> x0, local copies, waits for them, and re-layouts: 35.1 us -> none  [segment(): lax.map(lambda head_block: block_forward(head_block, input_rows, output_r...]
    dynamic_update_slice x25 -> x0, other arithmetic: 29.4 us -> none  [segment(): lax.map(lambda head_block: block_forward(head_block, input_rows, output_r...]
    pallas_call x0 -> x3, Pallas kernels: none -> 29.4 us  [the longest x1 12.2 us: on_device(): pl.pallas_call(functools.partial(carried_kernel, n, per, width), grid=gri...]
    another operation x50 -> x0, other arithmetic: 25.7 us -> none
    select_n x8 -> x0, other arithmetic: 23.6 us -> none  [turn(): return jax.tree.map(lambda a, b: jnp.where(reached, a, b), new, before)]
  transfers between devices with their start and end apart: 2 -> 3, of which waited for: 1 -> 3; matrix products, arithmetic and copies ran while one was open for 26% -> 0% of each run, Pallas kernels for 0% -> 7%
where the time goes in v1:
time: 131 us; the launch traced here: 130 us
  waiting for transfers between devices  50 us (38%)
  blocking collectives  40.2 us (31%)
  Pallas kernels  29.4 us (22%)
  starting transfers between devices  5.94 us (5%)
  local copies, waits for them, and re-layouts  4.28 us (3%)
    ppermute x3, waiting for transfers between devices, on_device(): lax.ppermute(sends[k - 1], 'seq', [(d, (d + k) % n) for d in range(n)])  50 us
    psum x1, blocking collectives, on_device(): total = lax.psum(param, ('seq', 'dp')) * factor  40.2 us
    pallas_call x1, Pallas kernels, on_device(): pl.pallas_call(functools.partial(carried_kernel, n, per, width), grid=gri...  12.2 us
    pallas_call x1, Pallas kernels, on_device(): pl.pallas_call(functools.partial(inside_kernel, per, width), grid=grid, i...  8.99 us
    pallas_call x1, Pallas kernels, on_device(): pl.pallas_call(functools.partial(state_kernel, n, per, width), grid=grid,...  8.24 us
    ppermute x3, starting transfers between devices, on_device(): lax.ppermute(sends[k - 1], 'seq', [(d, (d + k) % n) for d in range(n)])  5.94 us
    unnamed x6, local copies, waits for them, and re-layouts  3.76 us
  transfers between devices with their start and end apart: 3, of which 3 were waited for; matrix products, arithmetic and copies ran while one was open for 0% of the time, Pallas kernels for 7%

profile of v1, /device:TPU:0, one launch (start us, length us, event | category | flops | bytes accessed | tf_op | source)
XLA Modules:
  0.0 130.5 jit_solution(17826165467695693055)
XLA Ops:
  0.6 1.5 %copy.15 = bf16[1,256,40]{2,1,0:T(8,128)(2,1)} copy(bf16[1,256,40]{1,2,0:T(8,128)(2,1)} %param.9) | data formatting | bytes 40960 | tf_op args[1]
  2.1 8.2 %states.1 = (f32[136,2560]{1,0:T(8,128)}, f32[136,2560]{1,0:T(8,128)}, f32[136,2560]{1,0:T(8,128)}, f32[256,128]{1,0:T(8,128)}, f32[256,128]{1,0:T(8,128)}, /*in...) custom-call(s32[1]{0:T(128)} %bitcast.me_ref, bf16[256,40]{1,0:T(8,128)(2,1)} %bitcast.30, ...), custom_call_target="tpu_custom_call" | custom-call | tf_op jit(solution)/shard_map/states/pallas_call | solution.py:308
  10.3 3.0 %collective-permute-start = (f32[136,2560]{1,0:T(8,128)}, f32[136,2560]{1,0:T(8,128)S(1)}, u32[]{:S(2)}, u32[]{:S(2)}) collective-permute-start(f32[136,2560]{1,0:T(8,128)} %get-tuple-element.35), channel_id=1, source_target_pairs={{0,8},{8,16},{16,24},{24,0},{1,9},{9,17},{17,25},{25,1},{2,10},{10... | collective-permute-start | bytes 4177928 | tf_op jit(solution)/shard_map/ppermute | solution.py:324
  13.3 1.5 %collective-permute-start.1 = (f32[136,2560]{1,0:T(8,128)}, f32[136,2560]{1,0:T(8,128)S(1)}, u32[]{:S(2)}, u32[]{:S(2)}) collective-permute-start(f32[136,2560]{1,0:T(8,128)} %get-tuple-element.36), channel_id=1, source_target_pairs={{0,16},{8,24},{16,0},{24,8},{1,17},{9,25},{17,1},{25,9},{2,18},{10... | collective-permute-start | bytes 4177928 | tf_op jit(solution)/shard_map/ppermute | solution.py:324
  14.8 1.4 %collective-permute-start.2 = (f32[136,2560]{1,0:T(8,128)}, f32[136,2560]{1,0:T(8,128)}, u32[]{:S(2)}, u32[]{:S(2)}) collective-permute-start(f32[136,2560]{1,0:T(8,128)} %get-tuple-element.37), channel_id=1, source_target_pairs={{0,24},{8,0},{16,8},{24,16},{1,25},{9,1},{17,9},{25,17},{2,26},{10... | collective-permute-start | bytes 4177928 | tf_op jit(solution)/shard_map/ppermute | solution.py:324
  16.3 9.0 %inside.1 = (f32[256,2560]{1,0:T(8,128)}, f32[40,256]{1,0:T(8,128)}, f32[256,128]{1,0:T(8,128)}, f32[256,128]{1,0:T(8,128)}) custom-call(f32[256,128]{1,0:T(8,128)} %get-tuple-element.25.run_ref, f32[128,256]{1,0:T(8,128)} %get-tuple-element.30.run_t_ref, f32[256,128]{1,0:T(8,128)} %get-tuple-element.26.dt_ref, bf16[256,128]{1,0:T(8,128)(2,1)} %bitcast.25, ...), custom_call_target="tpu_custom_call" | custom-call | flops 10000000000 | bytes 10000000 | tf_op jit(solution)/shard_map/inside/pallas_call | solution.py:327
  25.3 20.6 %collective-permute-done.refs_0_ = f32[136,2560]{1,0:T(8,128)S(1)} collective-permute-done((f32[136,2560]{1,0:T(8,128)}, f32[136,2560]{1,0:T(8,128)S(1)}, u32[]{:S(2)}, u32[]{:S(2)}) %collective-permute-start) | collective-permute-done | bytes 1392672 | tf_op jit(solution)/shard_map/ppermute | solution.py:324
  45.9 0.0 copy-start
  45.9 28.9 %collective-permute-done.1.refs_1_ = f32[136,2560]{1,0:T(8,128)S(1)} collective-permute-done((f32[136,2560]{1,0:T(8,128)}, f32[136,2560]{1,0:T(8,128)S(1)}, u32[]{:S(2)}, u32[]{:S(2)}) %collective-permute-start.1) | collective-permute-done | bytes 1392672 | tf_op jit(solution)/shard_map/ppermute | solution.py:324
  74.9 0.0 copy-start.1
  74.9 0.4 collective-permute-done.2.refs_2_
  75.3 0.0 copy-done
  75.3 0.7 copy-done.1
  76.0 12.2 %carried.1 = (bf16[256,2560]{1,0:T(8,128)(2,1)}, f32[256,40]{1,0:T(8,128)}, f32[256,128]{1,0:T(8,128)}, f32[256,128]{1,0:T(8,128)}, f32[8,128]{1,0:T(8,128)}) custom-call(s32[1]{0:T(128)} %bitcast.me_ref, f32[40]{0:T(128)} %skip_ref.1, f32[1,40]{1,0:T(1,128)} %bitcast.33, f32[256,128]{1,0:T(8,128)} %get-tuple-element.25.run_ref, ...), custom_call_target="tpu_custom_call" | custom-call | tf_op jit(solution)/shard_map/carried/pallas_call | solution.py:344
  88.1 1.6 %copy.16 = f32[1,256,40]{1,2,0:T(8,128)} copy(f32[1,256,40]{2,1,0:T(8,128)} %bitcast.31) | data formatting | bytes 81920
  89.7 40.2 %psum.7 = f32[8,128]{1,0:T(8,128)S(1)} all-reduce(f32[8,128]{1,0:T(8,128)} %get-tuple-element.42), channel_id=1, replica_groups=mesh['seq'=4,'dp'=8] {'seq','dp'}, use_global_device_ids=true, to_apply=%region_0.0 | all-reduce | flops 1024 | bytes 8192 | tf_op jit(solution)/shard_map/psum | solution.py:364
  130.0 0.5 slice_bitcast_fusion
  (1 shorter events, 0.0 us)
Async XLA Ops:
  10.3 35.6 %collective-permute-start = (f32[136,2560]{1,0:T(8,128)}, f32[136,2560]{1,0:T(8,128)S(1)}, u32[]{:S(2)}, u32[]{:S(2)}) collective-permute-start(f32[136,2560]{1,0:T(8,128)} %get-tuple-element.35), channel_id=1, source_target_pairs={{0,8},{8,16},{16,24},{24,0},{1,9},{9,17},{17,25},{25,1},{2,10},{10... | collective-permute-start | bytes 4177928 | tf_op jit(solution)/shard_map/ppermute | solution.py:324
  13.3 61.5 %collective-permute-start.1 = (f32[136,2560]{1,0:T(8,128)}, f32[136,2560]{1,0:T(8,128)S(1)}, u32[]{:S(2)}, u32[]{:S(2)}) collective-permute-start(f32[136,2560]{1,0:T(8,128)} %get-tuple-element.36), channel_id=1, source_target_pairs={{0,16},{8,24},{16,0},{24,8},{1,17},{9,25},{17,1},{25,9},{2,18},{10... | collective-permute-start | bytes 4177928 | tf_op jit(solution)/shard_map/ppermute | solution.py:324
  14.8 60.4 %collective-permute-start.2 = (f32[136,2560]{1,0:T(8,128)}, f32[136,2560]{1,0:T(8,128)}, u32[]{:S(2)}, u32[]{:S(2)}) collective-permute-start(f32[136,2560]{1,0:T(8,128)} %get-tuple-element.37), channel_id=1, source_target_pairs={{0,24},{8,0},{16,8},{24,16},{1,25},{9,1},{17,9},{25,17},{2,26},{10... | collective-permute-start | bytes 4177928 | tf_op jit(solution)/shard_map/ppermute | solution.py:324
  45.9 29.4 %copy-start = (f32[136,2560]{1,0:T(8,128)}, f32[136,2560]{1,0:T(8,128)S(1)}, u32[]{:S(2)}) copy-start(f32[136,2560]{1,0:T(8,128)S(1)} %collective-permute-done.refs_0_) | copy-start | bytes 4177924
  74.9 1.1 copy-start.1

commit v2 on v1

--- a/solution.py
+++ b/solution.py
@@ -12,7 +12,8 @@
 BF16 = jnp.bfloat16
 LANES = 128
 EXTRA = 8
-WIRE = jnp.float32
+WIRE = jnp.float16
+FLOOR = -1000.0
 
 
 def dot(a, b, dims=((1,), (0,))):
@@ -96,10 +97,13 @@
     states = bt_ref.shape[0]
     state = dot(bt_ref[...], x_hi) + dot(bt_ref[...], x_lo)
     grad = dot(ct_ref[...], g_hi) + dot(ct_ref[...], g_lo)
-    extra = expand(last, 0, per, width)
+    ends = jnp.maximum(expand(last, 0, per, width)[EXTRA - 1 : EXTRA], FLOOR)
+    p1, p2, p3 = (part.astype(F32) for part in split3(ends))
+    line = lax.broadcasted_iota(jnp.int32, (EXTRA, ends.shape[1]), 0)
+    extra = jnp.where(line == 0, p1, jnp.where(line == 1, p2, jnp.where(line == 2, p3, 0.0)))
     for k in range(1, n):
-        sends[k - 1][:states, :] = jnp.where(me + k < n, state, grad).astype(WIRE)
-        sends[k - 1][states:, :] = extra.astype(WIRE)
+        sends[k - 1][:states, :] = jnp.where(me + k < n, state, grad)
+        sends[k - 1][states:, :] = extra
 
 
 def inside_kernel(
@@ -203,8 +207,8 @@
         for j, slot in enumerate(order):
             take = jnp.where(j + 1 <= limit, 1.0, 0.0)
             block = arrived[slot]
-            total = total + (take * jnp.exp(passed)) * block[:states, :].astype(F32)
-            low = block[states : states + EXTRA, :].astype(F32)[EXTRA - 1 : EXTRA]
+            total = total + (take * jnp.exp(passed)) * block[:states, :]
+            low = jnp.sum(block[states : states + EXTRA, :], axis=0, keepdims=True)
             passed = passed + jnp.where(j + 1 <= limit, low, 0.0)
         return total
 
@@ -274,6 +278,61 @@
         )
 
 
+def sum_kernel(groups, n, factor, in_ref, out_ref, dp_slots, seq_slots, part, send_dp, recv_dp,
+               send_seq, recv_seq):
+    stages = (
+        ("dp", groups, in_ref, dp_slots, send_dp, recv_dp, part, 1.0),
+        ("seq", n, part, seq_slots, send_seq, recv_seq, out_ref, factor),
+    )
+    barrier = pltpu.get_barrier_semaphore()
+    for axis, size, *_ in stages:
+        me = lax.axis_index(axis)
+        for k in range(1, size):
+            pl.semaphore_signal(
+                barrier, inc=1, device_id={axis: lax.rem(me + k, size)},
+                device_id_type=pl.DeviceIdType.MESH,
+            )
+    pl.semaphore_wait(barrier, groups + n - 2)
+    for axis, size, src, slots, send, recv, dst, scale in stages:
+        me = lax.axis_index(axis)
+        copies = []
+        for k in range(1, size):
+            copy = pltpu.make_async_remote_copy(
+                src_ref=src, dst_ref=slots.at[me], send_sem=send.at[k], recv_sem=recv.at[k],
+                device_id={axis: lax.rem(me + k, size)}, device_id_type=pl.DeviceIdType.MESH,
+            )
+            copy.start()
+            copies.append(copy)
+        slots[me] = src[...]
+        for copy in copies:
+            copy.wait()
+        total = slots[0]
+        for j in range(1, size):
+            total = total + slots[j]
+        dst[...] = total * scale
+
+
+def sum_all(param, groups, n, factor):
+    vmem = pl.BlockSpec(memory_space=pltpu.VMEM)
+    return pl.pallas_call(
+        functools.partial(sum_kernel, groups, n, factor),
+        out_shape=jax.ShapeDtypeStruct(param.shape, F32),
+        in_specs=[vmem],
+        out_specs=vmem,
+        scratch_shapes=[
+            pltpu.VMEM((groups,) + param.shape, F32),
+            pltpu.VMEM((n,) + param.shape, F32),
+            pltpu.VMEM(param.shape, F32),
+            pltpu.SemaphoreType.DMA((groups,)),
+            pltpu.SemaphoreType.DMA((groups,)),
+            pltpu.SemaphoreType.DMA((n,)),
+            pltpu.SemaphoreType.DMA((n,)),
+        ],
+        compiler_params=pltpu.CompilerParams(collective_id=0, has_side_effects=True),
+        name="sums",
+    )(param)
+
+
 def whole(shape):
     return pl.BlockSpec(shape, lambda i: tuple(0 for _ in shape))
 
@@ -311,7 +370,7 @@
         in_specs=[smem, whole((length, heads)), whole((1, heads)), whole((1, heads)),
                   whole((length, states)), whole((length, states)), cols, cols],
         out_specs=[message] * (n - 1) + rows * 2 + [whole((LANES, length))] + rows * 3,
-        out_shape=[jax.ShapeDtypeStruct((tall, channels), WIRE)] * (n - 1)
+        out_shape=[jax.ShapeDtypeStruct((tall, channels), F32)] * (n - 1)
         + [scalars, scalars, jax.ShapeDtypeStruct((LANES, length), F32)] + [scalars] * 3,
         scratch_shapes=[pltpu.VMEM((length, LANES), F32), pltpu.VMEM((states, length), BF16),
                         pltpu.VMEM((states, length), BF16)],
@@ -321,7 +380,7 @@
     sends = made[: n - 1]
     dt, run, run_t, sig, into, grow = made[n - 1 :]
     arrived = [
-        lax.ppermute(sends[k - 1], "seq", [(d, (d + k) % n) for d in range(n)])
+        lax.ppermute(sends[k - 1].astype(WIRE), "seq", [(d, (d + k) % n) for d in range(n)])
         for k in range(1, n)
     ]
     gx, inner, db_in, dc_in = pl.pallas_call(
@@ -360,8 +419,8 @@
         compiler_params=params,
         name="carried",
     )(me, skip_gain, rate_row, run, dt, sig, into, grow, b, c, inner, db_in, dc_in, x, g, gx,
-      *arrived)
-    total = lax.psum(param, ("seq", "dp")) * factor
+      *[part.astype(F32) for part in arrived])
+    total = sum_all(param, groups, n, factor)
     return (
         grad_tokens[None],
         grad_steps[None],

time: 131 us -> 78.4 us (0.60)
  blocking collectives: 40.2 us -> 0 us
  waiting for transfers between devices: 50 us -> 20.5 us
  Pallas kernels: 29.4 us -> 40.6 us
  other arithmetic: 0.01 us -> 6.57 us
    psum x1 -> x0, blocking collectives: 40.2 us -> none  [on_device(): total = lax.psum(param, ('seq', 'dp')) * factor]
    ppermute x3, waiting for transfers between devices: 50 us -> 20.5 us  [on_device(): lax.ppermute(sends[k - 1].astype(WIRE), 'seq', [(d, (d + k) % n) for d in...]
    pallas_call x0 -> x1, Pallas kernels: none -> 11.2 us  [sum_all(): pl.pallas_call(functools.partial(sum_kernel, groups, n, factor), out_shap...]
    convert_element_type x0 -> x6, other arithmetic: none -> 6.57 us  [the longest x3 4.9 us: on_device(): part.astype(F32)]
  transfers between devices with their start and end apart: 3 -> 3, of which waited for: 3 -> 2; matrix products, arithmetic and copies ran while one was open for 0% -> 3% of each run, Pallas kernels for 7% -> 12%
where the time goes in v2:
time: 78.4 us; the launch traced here: 77.9 us
  Pallas kernels  40.6 us (52%)
  waiting for transfers between devices  20.5 us (26%)
  other arithmetic  6.57 us (8%)
  starting transfers between devices  5.19 us (7%)
  local copies, waits for them, and re-layouts  4.39 us (6%)
    ppermute x3, waiting for transfers between devices, on_device(): lax.ppermute(sends[k - 1].astype(WIRE), 'seq', [(d, (d + k) % n) for d in...  20.5 us
    pallas_call x1, Pallas kernels, on_device(): pl.pallas_call(functools.partial(carried_kernel, n, per, width), grid=gri...  12.1 us
    pallas_call x1, Pallas kernels, sum_all(): pl.pallas_call(functools.partial(sum_kernel, groups, n, factor), out_shap...  11.2 us
    pallas_call x1, Pallas kernels, on_device(): pl.pallas_call(functools.partial(inside_kernel, per, width), grid=grid, i...  8.99 us
    pallas_call x1, Pallas kernels, on_device(): pl.pallas_call(functools.partial(state_kernel, n, per, width), grid=grid,...  8.22 us
    ppermute x3, starting transfers between devices, on_device(): lax.ppermute(sends[k - 1].astype(WIRE), 'seq', [(d, (d + k) % n) for d in...  5.19 us
    convert_element_type x3, other arithmetic, on_device(): part.astype(F32)  4.9 us
    unnamed x6, local copies, waits for them, and re-layouts  3.07 us
  transfers between devices with their start and end apart: 3, of which 2 were waited for; matrix products, arithmetic and copies ran while one was open for 3% of the time, Pallas kernels for 12%

profile of v2, /device:TPU:0, one launch (start us, length us, event | category | flops | bytes accessed | tf_op | source)
XLA Modules:
  0.0 77.9 jit_solution(2487841942177832867)
XLA Ops:
  0.6 1.5 %copy.15 = bf16[1,256,40]{2,1,0:T(8,128)(2,1)} copy(bf16[1,256,40]{1,2,0:T(8,128)(2,1)} %param.9) | data formatting | bytes 40960 | tf_op args[1]
  2.1 8.2 %states.1 = (f32[136,2560]{1,0:T(8,128)}, f32[136,2560]{1,0:T(8,128)}, f32[136,2560]{1,0:T(8,128)}, f32[256,128]{1,0:T(8,128)}, f32[256,128]{1,0:T(8,128)}, /*in...) custom-call(s32[1]{0:T(128)} %bitcast.me_ref, bf16[256,40]{1,0:T(8,128)(2,1)} %bitcast.30, ...), custom_call_target="tpu_custom_call" | custom-call | tf_op jit(solution)/shard_map/states/pallas_call | solution.py:367
  10.3 0.0 copy-start.1
  10.3 1.5 %convert_element_type.22 = f16[136,2560]{1,0:T(8,128)(2,1)S(1)} convert(f32[136,2560]{1,0:T(8,128)} %get-tuple-element.37) | non-fusion elementwise | flops 348160 | bytes 2088960 | tf_op jit(solution)/shard_map/convert_element_type | solution.py:383
  11.9 0.0 copy-start
  11.9 4.0 %collective-permute-start.2 = (f16[136,2560]{1,0:T(8,128)(2,1)S(1)}, f16[136,2560]{1,0:T(8,128)(2,1)S(1)}, u32[]{:S(2)}, u32[]{:S(2)}) collective-permute-start(f16[136,2560]{1,0:T(8,128)(2,1)S(1)} %convert_element_type.22), channel_id=1, source_target_pairs={{0,24},{8,0},{16,8},{24,16},{1,25},{9,1},{17,9},{25,17},{2,26},{10... | collective-permute-start | bytes 2088968 | tf_op jit(solution)/shard_map/ppermute | solution.py:383
  15.8 0.0 copy-done.1
  15.8 0.1 convert_element_type.20
  15.9 0.6 collective-permute-start.1
  16.5 0.0 copy-done
  16.5 0.1 convert_element_type.18
  16.6 0.6 collective-permute-start
  17.2 9.0 %inside.1 = (f32[256,2560]{1,0:T(8,128)}, f32[40,256]{1,0:T(8,128)}, f32[256,128]{1,0:T(8,128)}, f32[256,128]{1,0:T(8,128)}) custom-call(f32[256,128]{1,0:T(8,128)} %get-tuple-element.25.run_ref, f32[128,256]{1,0:T(8,128)} %get-tuple-element.30.run_t_ref, f32[256,128]{1,0:T(8,128)} %get-tuple-element.26.dt_ref, bf16[256,128]{1,0:T(8,128)(2,1)} %bitcast.25, ...), custom_call_target="tpu_custom_call" | custom-call | flops 10000000000 | bytes 10000000 | tf_op jit(solution)/shard_map/inside/pallas_call | solution.py:386
  26.2 5.6 %collective-permute-done.2 = f16[136,2560]{1,0:T(8,128)(2,1)S(1)} collective-permute-done((f16[136,2560]{1,0:T(8,128)(2,1)S(1)}, f16[136,2560]{1,0:T(8,128)(2,1)S(1)}, u32[]{:S(2)}, u32[]{:S(2)}) %collective-permute-start.2) | collective-permute-done | bytes 696352 | tf_op jit(solution)/shard_map/ppermute | solution.py:383
  31.8 1.3 %convert_element_type.23.refs_2_ = f32[136,2560]{1,0:T(8,128)} convert(f16[136,2560]{1,0:T(8,128)(2,1)S(1)} %collective-permute-done.2) | non-fusion elementwise | flops 348160 | bytes 2088960 | tf_op jit(solution)/shard_map/convert_element_type | solution.py:422
  33.1 14.9 %collective-permute-done.1 = f16[136,2560]{1,0:T(8,128)(2,1)S(1)} collective-permute-done((f16[136,2560]{1,0:T(8,128)(2,1)S(1)}, f16[136,2560]{1,0:T(8,128)(2,1)S(1)}, u32[]{:S(2)}, u32[]{:S(2)}) %collective-permute-start.1) | collective-permute-done | bytes 696352 | tf_op jit(solution)/shard_map/ppermute | solution.py:383
  48.0 1.3 %convert_element_type.21.refs_1_ = f32[136,2560]{1,0:T(8,128)} convert(f16[136,2560]{1,0:T(8,128)(2,1)S(1)} %collective-permute-done.1) | non-fusion elementwise | flops 348160 | bytes 2088960 | tf_op jit(solution)/shard_map/convert_element_type | solution.py:422
  49.3 0.0 collective-permute-done
  49.3 2.4 %convert_element_type.19.refs_0_ = f32[136,2560]{1,0:T(8,128)} convert(f16[136,2560]{1,0:T(8,128)(2,1)} %collective-permute-done) | non-fusion elementwise | flops 348160 | bytes 2088960 | tf_op jit(solution)/shard_map/convert_element_type | solution.py:422
  51.6 12.1 %carried.1 = (bf16[256,2560]{1,0:T(8,128)(2,1)}, f32[256,40]{1,0:T(8,128)}, f32[256,128]{1,0:T(8,128)}, f32[256,128]{1,0:T(8,128)}, f32[8,128]{1,0:T(8,128)}) custom-call(s32[1]{0:T(128)} %bitcast.me_ref, f32[40]{0:T(128)} %skip_ref.1, f32[1,40]{1,0:T(1,128)} %bitcast.33, f32[256,128]{1,0:T(8,128)} %get-tuple-element.25.run_ref, ...), custom_call_target="tpu_custom_call" | custom-call | tf_op jit(solution)/shard_map/carried/pallas_call | solution.py:403
  63.8 1.6 %copy.16 = f32[1,256,40]{1,2,0:T(8,128)} copy(f32[1,256,40]{2,1,0:T(8,128)} %bitcast.31) | data formatting | bytes 81920
  65.4 11.2 %sums.1 = f32[8,128]{1,0:T(8,128)} custom-call(f32[8,128]{1,0:T(8,128)} %get-tuple-element.42.in_ref), custom_call_target="tpu_custom_call" | custom-call | tf_op jit(solution)/shard_map/sums/pallas_call | solution.py:317
  76.6 1.3 %slice_bitcast_fusion = (f32[40]{0:T(128)}, f32[40]{0:T(128)}, f32[40]{0:T(128)}) fusion(f32[8,128]{1,0:T(8,128)} %sums.1), kind=kLoop, calls=%fused_computation | loop fusion | bytes 960 | tf_op jit(solution)/shard_map/squeeze | solution.py:431
Async XLA Ops:
  10.3 5.5 %copy-start.1 = (f32[136,2560]{1,0:T(8,128)S(1)}, f32[136,2560]{1,0:T(8,128)}, u32[]{:S(2)}) copy-start(f32[136,2560]{1,0:T(8,128)} %get-tuple-element.36) | copy-start | bytes 4177924
  11.9 4.6 %copy-start = (f32[136,2560]{1,0:T(8,128)S(1)}, f32[136,2560]{1,0:T(8,128)}, u32[]{:S(2)}) copy-start(f32[136,2560]{1,0:T(8,128)} %get-tuple-element.35) | copy-start | bytes 4177924
  11.9 20.0 %collective-permute-start.2 = (f16[136,2560]{1,0:T(8,128)(2,1)S(1)}, f16[136,2560]{1,0:T(8,128)(2,1)S(1)}, u32[]{:S(2)}, u32[]{:S(2)}) collective-permute-start(f16[136,2560]{1,0:T(8,128)(2,1)S(1)} %convert_element_type.22), channel_id=1, source_target_pairs={{0,24},{8,0},{16,8},{24,16},{1,25},{9,1},{17,9},{25,17},{2,26},{10... | collective-permute-start | bytes 2088968 | tf_op jit(solution)/shard_map/ppermute | solution.py:383
  15.9 32.1 %collective-permute-start.1 = (f16[136,2560]{1,0:T(8,128)(2,1)S(1)}, f16[136,2560]{1,0:T(8,128)(2,1)S(1)}, u32[]{:S(2)}, u32[]{:S(2)}) collective-permute-start(f16[136,2560]{1,0:T(8,128)(2,1)S(1)} %convert_element_type.20), channel_id=1, source_target_pairs={{0,16},{8,24},{16,0},{24,8},{1,17},{9,25},{17,1},{25,9},{2,18},{10... | collective-permute-start | bytes 2088968 | tf_op jit(solution)/shard_map/ppermute | solution.py:383
  16.6 32.7 %collective-permute-start = (f16[136,2560]{1,0:T(8,128)(2,1)S(1)}, f16[136,2560]{1,0:T(8,128)(2,1)}, u32[]{:S(2)}, u32[]{:S(2)}) collective-permute-start(f16[136,2560]{1,0:T(8,128)(2,1)S(1)} %convert_element_type.18), channel_id=1, source_target_pairs={{0,8},{8,16},{16,24},{24,0},{1,9},{9,17},{17,25},{25,1},{2,10},{10... | collective-permute-start | bytes 2088968 | tf_op jit(solution)/shard_map/ppermute | solution.py:383
